TPU v7x, 8 devices: a whole 2x2x1 slice. The times are simulated.
8 devices in a mesh: dp: 1 (over z), fsdp: 8 (over y, x, core).
Axes of the slice: x: 2, y: 2, z: 1, core: 2. Of those that a mesh axis runs over, the one named last changes fastest.
Arguments:
- dec_in: bfloat16 [64, 192, 4096], P(('dp', 'fsdp'))
- enc_out: bfloat16 [64, 384, 4096], P(('dp', 'fsdp'))
- dec_mask: int32 [64, 192], P(('dp', 'fsdp'))
- enc_mask: int32 [64, 384], P(('dp', 'fsdp'))
- rel_bias: float32 [32, 64], replicated
- norm_self: bfloat16 [4096], P('fsdp')
- self_q: bfloat16 [4096, 4096], P('fsdp')
- self_k: bfloat16 [4096, 4096], P('fsdp')
- self_v: bfloat16 [4096, 4096], P('fsdp')
- self_o: bfloat16 [4096, 4096], P('fsdp')
- norm_cross: bfloat16 [4096], P('fsdp')
- cross_q: bfloat16 [4096, 4096], P('fsdp')
- cross_k: bfloat16 [4096, 4096], P('fsdp')
- cross_v: bfloat16 [4096, 4096], P('fsdp')
- cross_o: bfloat16 [4096, 4096], P('fsdp')
- norm_ff: bfloat16 [4096], P('fsdp')
- ff_gate: bfloat16 [4096, 10240], P('fsdp')
- ff_lin: bfloat16 [4096, 10240], P('fsdp')
- ff_out: bfloat16 [10240, 4096], P('fsdp')
Outputs:
- output: bfloat16 [64, 192, 4096], P(('dp', 'fsdp'))
All inputs are finite; a program needn't handle non-finite values.
Results may differ from a plain program's by a relative error of at most 0.0177488.
Values are sent between devices in bfloat16 or wider.
A program may use at most 1 GiB of HBM per device.

v0:
```python
import math
import jax
import jax.numpy as jnp
from jax import lax
from jax.experimental import pallas as pl
from jax.experimental.pallas import tpu as pltpu
from jax.sharding import PartitionSpec as P

MESH = pl.DeviceIdType.MESH
F32, BF16 = jnp.float32, jnp.bfloat16
HEAD_DIM = 64
NUM_BUCKETS = 32
EXACT_BUCKETS = 16
MAX_DISTANCE = 128
NORM_EPS = 1e-6
MASK_FILL = -1e9
N_DEV = 8

AHEAD, PASS, DONE, RING = 4, 4, 5, 14
PARTNER, FIRST, REST, RELAY, SWAP_FIRST, SWAP, SWAP_D, KINDS = range(8)
TASKS = {'self_q': 8, 'self_k': 8, 'self_v': 8, 'self_o': 8, 'cross_k': 8, 'cross_v': 8, 'cross_q': 8, 'cross_o': 8, 'ff_gate': 20, 'ff_lin': 20, 'ff_out': 16}
ALL_TASKS = sum(TASKS.values())
TICKS = {'head': DONE + 2, 'self_q': 8, 'self_k': 8, 'self_v': 8, 'self_attend': 6, 'self_o': 6, 'cross_k0': 6, 'cross_k1': 5, 'cross_v0': 6, 'cross_v1': 5,
         'cross_q': 6, 'cross_attend': 10, 'cross_o': 6, 'ff_gate': 12, 'ff_lin': 10}
assert sum(TICKS.values()) == ALL_TASKS - TASKS['ff_out'] + DONE
ROW_BLOCK = 512
GROUP = 512


def bucket_ids(length):
    return [offset if offset < EXACT_BUCKETS else min(NUM_BUCKETS - 1, EXACT_BUCKETS + int(math.log(offset / EXACT_BUCKETS) / math.log(MAX_DISTANCE / EXACT_BUCKETS) * (NUM_BUCKETS - EXACT_BUCKETS))) for offset in range(length)]


def bucket_starts(length):
    ids = bucket_ids(length)
    return [next(n for n in range(length) if ids[n] >= b) for b in range(1, ids[-1] + 1)]


class Weight:
    def __init__(self, first, count, shard, got):
        self.first, self.count, self.shard, self.got = first, count, shard, got
        self.rows, self.width = shard.shape[0], shard.shape[1] // count


def layer_kernel(batch, names, rel_in, dec_mask_in, enc_mask_in, norm_ref, dec_ref, enc_ref, *refs):
    n_w = len(names)
    shards, refs = refs[:n_w], refs[n_w:]
    out_ref, q_ref, k_ref, v_ref, c_ref, ck_ref, cv_ref, g_ref, z_ref = refs[:9]
    gots, refs = refs[9:9 + n_w], refs[9 + n_w:]
    x_s, big, bias_s, dist_s, gain_in, gains, rel_ref, dec_mask_ref, enc_mask_ref, send_sem, recv_sem, norm_send, norm_recv, load_sem, small_sem = refs

    me = lax.axis_index('fsdp')
    weights, first = {}, 0
    for name, shard, got in zip(names, shards, gots):
        weights[name] = Weight(first, TASKS[name], shard, got)
        first += TASKS[name]
    rows, width = dec_ref.shape
    tgt = rows // batch
    src = enc_ref.shape[0] // batch
    row_block = min(ROW_BLOCK, rows)

    def remote(src_ref, dst_ref, kind, ring, bit):
        return pltpu.make_async_remote_copy(src_ref=src_ref, dst_ref=dst_ref, send_sem=send_sem.at[ring], recv_sem=recv_sem.at[kind, ring],
                                            device_id={'fsdp': me ^ bit}, device_id_type=MESH)

    class Task:
        def __init__(self, w, m, ring):
            cols = pl.ds(pl.multiple_of(m * w.width, w.width), w.width)
            own = w.shard.at[:, cols]
            slot = lambda j: w.got.at[j - 1, :, cols]
            bottom, top = pl.ds(0, w.rows // 2), pl.ds(w.rows // 2, w.rows // 2)
            low = lambda j: w.got.at[j - 1, bottom, cols]
            high = lambda j: w.got.at[j - 1, top, cols]
            self.to_partner = lambda: remote(own, slot(1), PARTNER, ring, 1)
            self.first_x = lambda: remote(w.shard.at[bottom, cols], low(2), FIRST, ring, 2)
            self.first_y = lambda: remote(w.shard.at[top, cols], high(4), FIRST, ring, 4)
            self.rest_x = lambda: remote(w.shard.at[top, cols], high(2), REST, ring, 2)
            self.rest_y = lambda: remote(w.shard.at[bottom, cols], low(4), REST, ring, 4)
            self.relay_y = lambda: remote(low(2), low(6), RELAY, ring, 4)
            self.relay_x = lambda: remote(high(4), high(6), RELAY, ring, 2)
            self.swap_x = lambda: remote(slot(2), slot(3), SWAP, ring, 1)
            self.swap_y = lambda: remote(slot(4), slot(5), SWAP, ring, 1)
            self.swap_d = lambda: remote(slot(6), slot(7), SWAP_D, ring, 1)
            self.swap_first_x = lambda: remote(low(2), low(3), SWAP_FIRST, ring, 1)
            self.swap_first_y = lambda: remote(high(4), high(5), SWAP_FIRST, ring, 1)
            self.swap_rest_x = lambda: remote(high(2), high(3), SWAP, ring, 1)
            self.swap_rest_y = lambda: remote(low(4), low(5), SWAP, ring, 1)
            self.halves = w is weights['ff_out']
            shape = lambda slots: w.got.at[pl.ds(0, slots), :, cols]
            self.got_all = lambda kind, slots: remote(shape(slots), shape(slots), kind, ring, 1).wait_recv()
            self.sent_all = lambda: remote(shape(7), shape(7), PARTNER, ring, 1).wait_send()

    def send(t):
        for copy in (t.first_x, t.first_y, t.to_partner):
            copy().start()

    def arrive(t):
        t.to_partner().wait_recv()
        t.got_all(FIRST, 1)
        for copy in (t.relay_y, t.relay_x, t.rest_y, t.rest_x, *((t.swap_first_x, t.swap_first_y) if t.halves else ())):
            copy().start()

    def pass_on_diagonal(t):
        t.got_all(RELAY, 1)
        t.swap_d().start()

    def pass_on_rest(t):
        t.got_all(REST, 1)
        for copy in (t.swap_rest_x, t.swap_rest_y) if t.halves else (t.swap_x, t.swap_y):
            copy().start()

    def pass_on(t):
        pass_on_diagonal(t)
        pass_on_rest(t)

    def finish(t):
        t.swap_d().wait_recv()
        t.got_all(SWAP, 2)
        t.sent_all()

    def on_task(t, low, high, act, among=None, stop=ALL_TASKS):
        for w in among or weights.values():
            last = min(w.first + w.count, stop)
            if low < last and w.first < high:
                def run(w=w):
                    act(Task(w, t - w.first, lax.rem(t, RING)))
                if w.first <= low and high <= last:
                    run()
                else:
                    pl.when((t >= w.first) & (t < last))(run)

    streamed = [w for name, w in weights.items() if name != 'ff_out']
    out_look = weights['ff_out'].first + PASS

    def tick(i, low, high):
        on_task(i, low, high, arrive, stop=out_look)
        on_task(i + AHEAD, low + AHEAD, high + AHEAD, send, stop=out_look + AHEAD)
        on_task(i - PASS, low - PASS, high - PASS, pass_on, streamed)
        on_task(i - DONE, low - DONE, high - DONE, finish, streamed)

    done = [0]

    def stage_ticks(name):
        low, count = done[0], TICKS[name]
        done[0] = low + count
        return low, count

    def ticks_before(plan, n, steps, least=min):
        low, count = plan
        spread = steps if count == steps else max(steps - 4, 1)
        return low + least((n * count) // spread, count)

    def run_ticks(plan, n, steps):
        with jax.named_scope('ticks'):
            @pl.loop(ticks_before(plan, n, steps, jnp.minimum), ticks_before(plan, n + 1, steps, jnp.minimum))
            def _(i):
                tick(i, plan[0], plan[0] + plan[1])

    def load(src_ref, dst_ref):
        copy = pltpu.make_async_copy(src_ref, dst_ref, load_sem)
        copy.start()
        copy.wait()

    def norm(which):
        @pl.loop(0, rows // 16)
        def _(r):
            span = pl.ds(pl.multiple_of(r * 16, 16), 16)
            v = x_s[span, :].astype(F32)
            scale = lax.rsqrt(jnp.mean(v * v, axis=-1, keepdims=True) + NORM_EPS)
            big[span, pl.ds(0, width)] = (v * scale * gains[pl.ds(which, 1), :]).astype(BF16)

    def matmul(name, stage, split, store, in_specs=(), ins=(), out_specs=(), outs=()):
        w = weights[name]
        steps, cols = w.count * split, w.width // split
        plan = stage_ticks(stage)
        for n in range(steps):
            assert ticks_before(plan, n, steps) > w.first + min(n + 1, steps - 1) // split + DONE

        def body(own, got, *rest):
            n = pl.program_id(0)

            @pl.loop(0, rows // row_block)
            def _(m):
                span = pl.ds(pl.multiple_of(m * row_block, row_block), row_block)
                total = None
                for j in range(N_DEV):
                    part = big[span, pl.ds(pl.multiple_of((me ^ j) * w.rows, 128), w.rows)]
                    term = jnp.dot(part, own[...] if j == 0 else got[j - 1], preferred_element_type=F32)
                    total = term if total is None else total + term
                store(total, span, n, *rest)

            run_ticks(plan, n, steps)

        with jax.named_scope(stage):
            pltpu.emit_pipeline(
                body, grid=(steps,),
                in_specs=[pl.BlockSpec((w.rows, cols), lambda n: (0, n)), pl.BlockSpec((N_DEV - 1, w.rows, cols), lambda n: (0, 0, n)), *in_specs],
                out_specs=list(out_specs))(w.shard, w.got, *ins, *outs)

    def project(name, stage, dst_ref, half=0):
        cols = weights[name].width

        def store(total, span, n, dst):
            dst[span, :] = total.astype(BF16)

        matmul(name, stage, 1, store, out_specs=[pl.BlockSpec((rows, cols), lambda n: (half, n))], outs=[dst_ref])

    def residual(name, stage):
        cols = weights[name].width

        def store(total, span, n):
            where = (span, pl.ds(pl.multiple_of(n * cols, cols), cols))
            x_s[where] = (x_s[where].astype(F32) + total.astype(BF16).astype(F32)).astype(BF16)

        matmul(name, stage, 1, store)

    left = lax.broadcasted_iota(jnp.int32, (tgt, 2 * HEAD_DIM), 1) < HEAD_DIM

    def softmax(scores):
        e = jnp.exp(scores - jnp.max(scores, axis=-1, keepdims=True))
        return (e * (1.0 / jnp.sum(e, axis=-1, keepdims=True))).astype(BF16)

    def attend(stage, keys, k_src, v_src, prepare, mask_scores):
        group = min(GROUP, width)
        plan = stage_ticks(stage)
        steps = (width // group) * batch

        def body(q, k, v, c):
            g, b = pl.program_id(0), pl.program_id(1)
            prepare(g, b)
            for pair in range(group // (2 * HEAD_DIM)):
                cols = pl.ds(pair * 2 * HEAD_DIM, 2 * HEAD_DIM)
                q_pair = q[:, cols].astype(F32)
                both = jnp.concatenate([jnp.where(left, q_pair, 0.0), jnp.where(left, 0.0, q_pair)], 0).astype(BF16)
                scores = lax.dot_general(both, k[:, cols], (((1,), (1,)), ((), ())), preferred_element_type=F32)
                prob = jnp.concatenate([softmax(mask_scores(scores[h * tgt:(h + 1) * tgt], 2 * pair + h, b)) for h in range(2)], 0)
                ctx = jnp.dot(prob, v[:, cols], preferred_element_type=F32)
                c[:, cols] = jnp.where(left, ctx[:tgt], ctx[tgt:]).astype(BF16)
            run_ticks(plan, g * batch + b, steps)

        spec = lambda length: pl.BlockSpec((length, group), lambda g, b: (b, g))
        with jax.named_scope(stage):
            pltpu.emit_pipeline(body, grid=(width // group, batch), in_specs=[spec(tgt), spec(keys), spec(keys)], out_specs=[spec(tgt)])(q_ref, k_src, v_src, c_ref)

    def self_attention():
        heads = min(GROUP, width) // HEAD_DIM
        causal = lax.broadcasted_iota(jnp.int32, (tgt, tgt), 1) <= lax.broadcasted_iota(jnp.int32, (tgt, tgt), 0)

        def prepare(g, b):
            @pl.when(b == 0)
            def _():
                @pl.loop(0, heads)
                def _(h):
                    row = jnp.broadcast_to(dist_s[pl.ds(g * heads + h, 1), :], (tgt, dist_s.shape[1]))
                    bias_s[h] = pltpu.roll(row, 0, 1, stride=1, stride_axis=0)[:, :tgt]

        def mask_scores(scores, h, b):
            allowed = causal & (dec_mask_ref[pl.ds(b, 1), :] > 0)
            return jnp.where(allowed, scores + bias_s[h], MASK_FILL)

        attend('self_attend', tgt, k_ref, v_ref, prepare, mask_scores)

    def cross_attention():
        def mask_scores(scores, h, b):
            return jnp.where(enc_mask_ref[pl.ds(b, 1), :] > 0, scores, MASK_FILL)

        attend('cross_attend', src, ck_ref, cv_ref, lambda g, b: None, mask_scores)

    hidden = big.at[:, pl.ds(0, width)]

    barrier = pltpu.get_barrier_semaphore()
    for j in range(1, N_DEV):
        pl.semaphore_signal(barrier, inc=1, device_id={'fsdp': me ^ j}, device_id_type=MESH)
    pl.semaphore_wait(barrier, N_DEV - 1)

    @pl.loop(0, AHEAD)
    def _(t):
        on_task(t, 0, AHEAD, send)

    def norm_copy(j):
        return pltpu.make_async_remote_copy(src_ref=norm_ref, dst_ref=gain_in.at[me], send_sem=norm_send.at[j], recv_sem=norm_recv.at[j],
                                            device_id={'fsdp': me ^ j}, device_id_type=MESH)

    for j in range(1, N_DEV):
        norm_copy(j).start()
    load_dec = pltpu.make_async_copy(dec_ref, x_s, load_sem)
    load_dec.start()
    load_norm = pltpu.make_async_copy(norm_ref, gain_in.at[me], norm_send.at[0])
    load_norm.start()
    small = [pltpu.make_async_copy(*pair, small_sem.at[k]) for k, pair in enumerate(((rel_in, rel_ref), (dec_mask_in, dec_mask_ref), (enc_mask_in, enc_mask_ref)))]
    for copy in small:
        copy.start()
    plan = stage_ticks('head')

    def head_ticks(begin, end):
        with jax.named_scope('head'):
            @pl.loop(begin, end)
            def _(i):
                tick(i, plan[0], plan[0] + plan[1])

    head_ticks(0, 2)
    for copy in small:
        copy.wait()
    lanes = dist_s.shape[1]
    row = lax.broadcasted_iota(jnp.int32, (lanes, rel_ref.shape[1]), 0)
    distance = jnp.where(row == 0, 0, lanes - row)
    table = jnp.broadcast_to(rel_ref[0:1, :], row.shape)
    for b, start in enumerate(bucket_starts(tgt)):
        table = jnp.where(distance >= start, rel_ref[b + 1:b + 2, :], table)
    dist_s[...] = table.T
    head_ticks(2, 4)
    for j in range(1, N_DEV):
        norm_copy(j).wait()
    load_norm.wait()
    per = width // N_DEV
    for d in range(N_DEV):
        gains[:, d * per:(d + 1) * per] = gain_in[d]
    load_dec.wait()
    norm(0)
    head_ticks(4, plan[1])

    project('self_q', 'self_q', q_ref)
    project('self_k', 'self_k', k_ref)
    project('self_v', 'self_v', v_ref)
    self_attention()
    load(c_ref, hidden)
    residual('self_o', 'self_o')
    for name, dst in (('cross_k', ck_ref), ('cross_v', cv_ref)):
        for half in range(2):
            load(enc_ref.at[pl.ds(half * rows, rows), :], hidden)
            project(name, f'{name}{half}', dst, half)
    norm(1)
    project('cross_q', 'cross_q', q_ref)
    cross_attention()
    load(c_ref, hidden)
    residual('cross_o', 'cross_o')
    norm(2)

    cols = weights['ff_gate'].width // 2
    block = pl.BlockSpec((rows, cols), lambda n: (0, n))

    def store_gate(total, span, n, g):
        g[span, :] = total.astype(BF16)

    def store_lin(total, span, n, g, z):
        act = jax.nn.gelu(g[span, :].astype(F32), approximate=True)
        z[span, :] = (act * total.astype(BF16).astype(F32)).astype(BF16)

    matmul('ff_gate', 'ff_gate', 2, store_gate, out_specs=[block], outs=[g_ref])
    matmul('ff_lin', 'ff_lin', 2, store_lin, in_specs=[block], ins=[g_ref], out_specs=[block], outs=[z_ref])
    load(z_ref, big)
    w = weights['ff_out']

    def ff_out_loop(early, late, total, outs, early_sem, late_sem, out_sem):
        cols, half = w.width, w.rows // 2
        direct = (2, 4, 3, 5)
        begins = lambda j, first: 0 if (j in (2, 3)) == first else half

        def span_of(m):
            return pl.ds(pl.multiple_of(m * row_block, row_block), row_block)

        def cols_of(n):
            return pl.ds(pl.multiple_of(n * cols, cols), cols)

        def product(span, parts):
            terms = [jnp.dot(big[span, pl.ds(pl.multiple_of((me ^ j) * w.rows + at, 128), size)], read(), preferred_element_type=F32) for j, at, size, read in parts]
            return sum(terms[1:], terms[0])

        def add(n, parts, new=False):
            @pl.loop(0, rows // row_block)
            def _(m):
                at = (lax.rem(n, 2), span_of(m), slice(None))
                part = product(span_of(m), parts)
                total[at] = part if new else total[at] + part

        def whole(p, j):
            return (j, 0, w.rows, lambda: early[p])

        def halves(n, first, which):
            return [(j, begins(j, first), half, lambda p=p, j=j: late[lax.rem(n, 2), p, pl.ds(begins(j, first), half), :]) for p, j in enumerate(direct) if j in which]

        def fetch(n, p, j):
            return pltpu.make_async_copy(w.shard.at[:, cols_of(n)] if j == 0 else w.got.at[j - 1, :, cols_of(n)], early.at[p], early_sem.at[p])

        def fetch_half(n, j, first):
            p, span = direct.index(j), pl.ds(begins(j, first), half)
            return pltpu.make_async_copy(w.got.at[j - 1, span, cols_of(n)], late.at[lax.rem(n, 2), p, span], late_sem.at[lax.rem(n, 2), 2 * p + int(first)])

        def out_copy(n):
            return pltpu.make_async_copy(outs.at[lax.rem(n, 2)], out_ref.at[:, cols_of(n)], out_sem.at[lax.rem(n, 2)])

        def task(n):
            return Task(w, n, lax.rem(w.first + n, RING))

        def fetch_early(n):
            for p in (0, 1):
                fetch(n, p, p).start()
            task(n).got_all(SWAP_FIRST, 1)
            for j in direct:
                fetch_half(n, j, True).start()

        def add_own(n):
            for p in (0, 1):
                fetch(n, p, p).wait()
            add(n, [whole(0, 0), whole(1, 1)], new=True)

        def add_first(n):
            for j in direct:
                fetch_half(n, j, True).wait()
            add(n, halves(n, True, direct))

        fetch_early(0)
        add_own(0)

        @pl.loop(0, w.count)
        def _(n):
            t = task(n)
            more = n < w.count - 1

            @pl.when(more)
            def _():
                fetch_early(n + 1)

            with jax.named_scope('wait_diagonal'):
                pass_on_diagonal(t)
            fetch(n, 2, 6).start()
            add_first(n)
            t.swap_d().wait_recv()
            fetch(n, 3, 7).start()
            for p, j in ((2, 6), (3, 7)):
                fetch(n, p, j).wait()
                add(n, [whole(p, j)])
            with jax.named_scope('wait_rest'):
                pass_on_rest(t)
            for j in (2, 4):
                fetch_half(n, j, False).start()
            pl.when(more)(lambda: add_own(n + 1))
            for j in (2, 4):
                fetch_half(n, j, False).wait()
            add(n, halves(n, False, (2, 4)))
            t.got_all(SWAP, 1)
            for j in (3, 5):
                fetch_half(n, j, False).start()

            @pl.when(n >= 2)
            def _():
                out_copy(n - 2).wait()

            for j in (3, 5):
                fetch_half(n, j, False).wait()

            @pl.loop(0, rows // row_block)
            def _(m):
                span = span_of(m)
                update = (total[lax.rem(n, 2), span, :] + product(span, halves(n, False, (3, 5)))).astype(BF16)
                outs[lax.rem(n, 2), span, :] = (x_s[span, cols_of(n)].astype(F32) + update.astype(F32)).astype(BF16)

            out_copy(n).start()
            t.sent_all()
            with jax.named_scope('ticks'):
                on_task(out_look + n, out_look, out_look + w.count, arrive, [w])
                on_task(out_look + AHEAD + n, out_look + AHEAD, out_look + AHEAD + w.count, send, [w])

            @pl.when(n == w.count - 1)
            def _():
                out_copy(n - 1).wait()
                out_copy(n).wait()

    dma = pltpu.SemaphoreType.DMA
    with jax.named_scope('ff_out'):
        pl.run_scoped(ff_out_loop, pltpu.VMEM((4, w.rows, w.width), BF16), pltpu.VMEM((2, 4, w.rows, w.width), BF16), pltpu.VMEM((2, rows, w.width), F32),
                      pltpu.VMEM((2, rows, w.width), BF16), dma((4,)), dma((2, 8)), dma((2,)))


def hand_on_kernel(src_ref, dst_ref, held, read_sem, write_sem):
    parts = read_sem.shape[0]
    size = src_ref.shape[0] // parts
    read = lambda k: pltpu.make_async_copy(src_ref.at[pl.ds(k * size, size)], held.at[pl.ds(k * size, size)], read_sem.at[k])
    write = lambda k: pltpu.make_async_copy(held.at[pl.ds(k * size, size)], dst_ref.at[pl.ds(k * size, size)], write_sem.at[k])
    for k in range(parts):
        read(k).start()
    for k in range(parts):
        read(k).wait()
        write(k).start()
    for k in range(parts):
        write(k).wait()


def hand_on(x):
    parts = 24
    any_spec, dma = pl.BlockSpec(memory_space=pl.ANY), pltpu.SemaphoreType.DMA
    return pl.pallas_call(hand_on_kernel, out_shape=jax.ShapeDtypeStruct(x.shape, x.dtype), in_specs=[any_spec], out_specs=any_spec,
                          scratch_shapes=[pltpu.VMEM(x.shape, x.dtype), dma((parts,)), dma((parts,))], name='hand_on')(x)


def local_layer(dec_in, enc_out, dec_mask, enc_mask, rel_bias, norm_self, self_q, self_k, self_v, self_o, norm_cross, cross_q, cross_k, cross_v, cross_o, norm_ff, ff_gate, ff_lin, ff_out):
    batch, tgt, width = dec_in.shape
    src = enc_out.shape[1]
    rows = batch * tgt
    given = dict(self_q=self_q, self_k=self_k, self_v=self_v, self_o=self_o, cross_k=cross_k, cross_v=cross_v, cross_q=cross_q, cross_o=cross_o, ff_gate=ff_gate, ff_lin=ff_lin, ff_out=ff_out)
    names = list(TASKS)
    shards = [given[n] for n in names]
    lanes = -(-2 * tgt // 128) * 128 if tgt % 128 == 0 else -(-(tgt + 1) // 128) * 128
    which = lax.broadcasted_iota(jnp.int32, (4, norm_self.shape[0]), 0)
    norms = jnp.where(which == 0, norm_self[None], jnp.where(which == 1, norm_cross[None], norm_ff[None])).astype(F32)
    any_spec = pl.BlockSpec(memory_space=pl.ANY)
    hbm = lambda *shape: jax.ShapeDtypeStruct(shape, BF16)
    ff = ff_gate.shape[1]
    heads = rel_bias.shape[1]
    outs = [hbm(rows, width)] + [hbm(rows, width)] * 4 + [hbm(batch * src, width)] * 2 + [hbm(rows, ff)] * 2 + [hbm(N_DEV - 1, *s.shape) for s in shards]
    dma = pltpu.SemaphoreType.DMA
    flops = 2 * rows * width * (6 * width + 3 * ff) + 4 * batch * src * width * width
    result = pl.pallas_call(
        lambda *refs: layer_kernel(batch, names, *refs),
        out_shape=outs,
        in_specs=[any_spec] * (6 + len(shards)),
        out_specs=[any_spec] * len(outs),
        scratch_shapes=[
            pltpu.VMEM((rows, width), BF16),
            pltpu.VMEM((rows, ff), BF16),
            pltpu.VMEM((min(GROUP, width) // HEAD_DIM, tgt, tgt), F32),
            pltpu.VMEM((heads, lanes), F32),
            pltpu.VMEM((N_DEV,) + norms.shape, F32),
            pltpu.VMEM((4, width), F32),
            pltpu.VMEM(rel_bias.shape, F32), pltpu.VMEM(dec_mask.shape, jnp.int32), pltpu.VMEM(enc_mask.shape, jnp.int32),
            dma((RING,)), dma((KINDS, RING)), dma((N_DEV,)), dma((N_DEV,)), dma(()), dma((3,)),
        ],
        compiler_params=pltpu.CompilerParams(collective_id=0, has_side_effects=True, vmem_limit_bytes=67_043_328),
        cost_estimate=pl.CostEstimate(flops=flops, bytes_accessed=20 * sum(s.size for s in shards), transcendentals=0),
        name='layer',
    )(rel_bias, dec_mask, enc_mask, norms, dec_in.reshape(rows, width), enc_out.reshape(batch * src, width), *shards)
    return hand_on(result[0]).reshape(dec_in.shape)


def solution(mesh):
    row_spec = P(('dp', 'fsdp'), None, None)
    mask_spec = P(('dp', 'fsdp'), None)
    weight_spec = P('fsdp', None)
    scale_spec = P('fsdp')
    in_specs = (row_spec, row_spec, mask_spec, mask_spec, P(None, None), scale_spec, weight_spec, weight_spec, weight_spec, weight_spec, scale_spec, weight_spec, weight_spec, weight_spec, weight_spec, scale_spec, weight_spec, weight_spec, weight_spec)
    return jax.shard_map(local_layer, mesh=mesh, in_specs=in_specs, out_specs=row_spec, check_vma=False)
```

profile of v0, /device:TPU:0, one launch (start us, length us, event | category | flops | bytes accessed | tf_op | source)
XLA Modules:
  0.0 2115.1 jit_solution(13007761990995474357)
XLA Ops:
  0.0 1.4 select_convert_fusion.refs_3_
  1.4 2104.1 %layer.1 = (bf16[1536,4096]{1,0:T(8,128)(2,1)}, bf16[1536,4096]{1,0:T(8,128)(2,1)}, bf16[1536,4096]{1,0:T(8,128)(2,1)}, bf16[1536,4096]{1,0:T(8,128)(2,1)}, bf16...) custom-call(f32[32,64]{1,0:T(8,128)} %refs_0_.1, ...), custom_call_target="tpu_custom_call" | custom-call | flops 901943132160 | bytes 650117120 | tf_op jit(solution)/shard_map/layer/pallas_call | solution.py:513
  2105.5 9.5 hand_on.1
  (1 shorter events, 0.0 us)
where the time goes:
time: 2120 us
  Pallas kernels  2110 us (100%)
    pallas_call x1, Pallas kernels, local_layer(): pl.pallas_call(lambda *refs: layer_kernel(batch, names, *refs), out_shape...  2100 us

commit v1 on v0

--- a/solution.py
+++ b/solution.py
@@ -487,7 +487,7 @@
 
 
 def hand_on(x):
-    parts = 24
+    parts = 8
     any_spec, dma = pl.BlockSpec(memory_space=pl.ANY), pltpu.SemaphoreType.DMA
     return pl.pallas_call(hand_on_kernel, out_shape=jax.ShapeDtypeStruct(x.shape, x.dtype), in_specs=[any_spec], out_specs=any_spec,
                           scratch_shapes=[pltpu.VMEM(x.shape, x.dtype), dma((parts,)), dma((parts,))], name='hand_on')(x)

time: 2120 us -> 2120 us (level)
  no operation moved by 1% of the time
where the time goes in v1:
time: 2120 us; the launch traced here: 2110 us
  Pallas kernels  2110 us (100%)
    pallas_call x1, Pallas kernels, local_layer(): pl.pallas_call(lambda *refs: layer_kernel(batch, names, *refs), out_shape...  2100 us

profile of v1, /device:TPU:0, one launch (start us, length us, event | category | flops | bytes accessed | tf_op | source)
XLA Modules:
  0.0 2115.0 jit_solution(9825751333266520215)
XLA Ops:
  0.0 1.4 select_convert_fusion.refs_3_
  1.4 2104.1 %layer.1 = (bf16[1536,4096]{1,0:T(8,128)(2,1)}, bf16[1536,4096]{1,0:T(8,128)(2,1)}, bf16[1536,4096]{1,0:T(8,128)(2,1)}, bf16[1536,4096]{1,0:T(8,128)(2,1)}, bf16...) custom-call(f32[32,64]{1,0:T(8,128)} %refs_0_.1, ...), custom_call_target="tpu_custom_call" | custom-call | flops 901943132160 | bytes 650117120 | tf_op jit(solution)/shard_map/layer/pallas_call | solution.py:513
  2105.5 9.3 hand_on.1
  (1 shorter events, 0.0 us)
